TPU v7x, 32 devices: a whole 2x2x4 slice. The times are simulated.
32 devices in a mesh: inl: 4 (over z), xln: 8 (over y, x, core).
Axes of the slice: x: 2, y: 2, z: 4, core: 2. Of those that a mesh axis runs over, the one named last changes fastest.
Arguments:
- noisy: float32 [128, 256, 512], P('inl', 'xln'), may hold values from -6 to 6
- bound: float32 [128, 256, 512], P('inl', 'xln'), may hold values from 0.05 to 0.5
Outputs:
- denoised: float32 [128, 256, 512], P('inl', 'xln')
- dual: float32 [3, 128, 256, 512], P(None, 'inl', 'xln')
- norms: float32 [2, 2], replicated
All inputs are finite; a program needn't handle non-finite values.
Results may differ from a plain program's by a relative error of at most 0.0001.
Values sent between devices are 32-bit elements; how exact they have to be, the bound alone decides.
A program may use at most 64 MiB of HBM per device.

v0:
```python
import jax
import jax.numpy as jnp
from jax import lax
from jax.sharding import PartitionSpec as P

ITERS = 2
SIGMA = 0.28
TAU = 0.28


def passed_along(value, axis, steps):
    count = lax.axis_size(axis)
    first, last = (max(0, -steps), min(count, count - steps))
    return lax.ppermute(value, axis, [(source, source + steps) for source in range(first, last)])


def depth_forward(field):
    return jnp.concatenate(
        [field[:, :, 1:] - field[:, :, :-1], jnp.zeros_like(field[:, :, :1])], axis=2
    )


def depth_backward(field):
    return field - jnp.concatenate([jnp.zeros_like(field[:, :, :1]), field[:, :, :-1]], axis=2)


def finish(sums_list):
    return jnp.sqrt(lax.psum(jnp.stack(sums_list), ("inl", "xln")))


def record(primal_sum, dual_sum, sums_list):
    sums_list.append(jnp.stack([primal_sum, dual_sum]))


def per_device(noisy, bound):
    sums_list = []
    inl_flag = (lax.axis_index("inl") < lax.axis_size("inl") - 1).astype(jnp.float32)
    xln_flag = (lax.axis_index("xln") < lax.axis_size("xln") - 1).astype(jnp.float32)
    primal = noisy
    smooth = noisy
    dual_i = jnp.zeros_like(noisy)
    dual_x = jnp.zeros_like(noisy)
    dual_z = jnp.zeros_like(noisy)
    for step in range(ITERS):
        next_i = passed_along(smooth[0:1], "inl", -1)
        next_x = passed_along(smooth[:, 0:1], "xln", -1)
        grad_i = jnp.concatenate(
            [smooth[1:] - smooth[:-1], (next_i - smooth[-1:]) * inl_flag], axis=0
        )
        grad_x = jnp.concatenate(
            [smooth[:, 1:] - smooth[:, :-1], (next_x - smooth[:, -1:]) * xln_flag], axis=1
        )
        fresh_i = jnp.clip(dual_i + SIGMA * grad_i, -bound, bound)
        fresh_x = jnp.clip(dual_x + SIGMA * grad_x, -bound, bound)
        fresh_z = jnp.clip(dual_z + SIGMA * depth_forward(smooth), -bound, bound)
        prev_i = passed_along(fresh_i[-1:], "inl", 1)
        prev_x = passed_along(fresh_x[:, -1:], "xln", 1)
        diverge = fresh_i - jnp.concatenate([prev_i, fresh_i[:-1]], axis=0)
        diverge = diverge + (fresh_x - jnp.concatenate([prev_x, fresh_x[:, :-1]], axis=1))
        diverge = diverge + depth_backward(fresh_z)
        updated = (primal + TAU * diverge + TAU * noisy) / (1.0 + TAU)
        primal_sum = jnp.sum((updated - primal) ** 2)
        dual_sum = (
            jnp.sum((fresh_i - dual_i) ** 2)
            + jnp.sum((fresh_x - dual_x) ** 2)
            + jnp.sum((fresh_z - dual_z) ** 2)
        )
        record(primal_sum, dual_sum, sums_list)
        smooth = 2.0 * updated - primal
        primal = updated
        dual_i, dual_x, dual_z = (fresh_i, fresh_x, fresh_z)
    norms = finish(sums_list)
    return (primal, jnp.stack([dual_i, dual_x, dual_z]), norms)


def solution(mesh):
    in_specs = (P("inl", "xln", None), P("inl", "xln", None))
    out_specs = (P("inl", "xln", None), P(None, "inl", "xln", None), P())
    return jax.shard_map(
        per_device, mesh=mesh, in_specs=in_specs, out_specs=out_specs, check_vma=False
    )
```

profile of v0, /device:TPU:0, one launch (start us, length us, event | category | flops | bytes accessed | tf_op | source)
XLA Modules:
  0.0 110.8 jit_solution(10471086511929388984)
XLA Ops:
  0.6 0.8 slice.92
  1.5 1.3 %collective-permute-start = (f32[1,32,512]{2,1,0:T(8,128)S(1)}, f32[1,32,512]{2,1,0:T(8,128)S(1)}, u32[]{:S(2)}, u32[]{:S(2)}) collective-permute-start(f32[1,32,512]{2,1,0:T(8,128)S(1)} %slice.92), channel_id=1, source_target_pairs={{8,0},{16,8},{24,16},{9,1},{17,9},{25,17},{10,2},{18,10},{26,18},{... | collective-permute-start | bytes 196616 | tf_op jit(solution)/shard_map/ppermute | solution.py:14
  2.8 1.1 slice.98
  3.9 1.4 %collective-permute-start.2 = (f32[32,1,512]{2,1,0:T(1,128)S(1)}, f32[32,1,512]{2,1,0:T(1,128)S(1)}, u32[]{:S(2)}, u32[]{:S(2)}) collective-permute-start(f32[32,1,512]{2,1,0:T(1,128)S(1)} %slice.98), channel_id=1, source_target_pairs={{1,0},{2,1},{3,2},{4,3},{5,4},{6,5},{7,6},{9,8},{10,9},{11,10},{12... | collective-permute-start | bytes 196616 | tf_op jit(solution)/shard_map/ppermute | solution.py:14
  5.3 4.1 %slice_subtract_fusion.3 = f32[32,31,512]{2,1,0:T(8,128)} fusion(f32[32,32,512]{2,1,0:T(8,128)} %param.2), kind=kLoop, calls=%fused_computation.44 | loop fusion | flops 507904 | bytes 6094848 | tf_op jit(solution)/shard_map/sub | solution.py:51
  9.4 2.0 %slice_subtract_fusion.2 = f32[32,32,511]{2,1,0:T(8,128)} fusion(f32[32,32,512]{2,1,0:T(8,128)S(1)} %copy-done), kind=kLoop, calls=%fused_computation.43 | loop fusion | flops 523264 | bytes 6279168 | tf_op jit(solution)/shard_map/sub | solution.py:19
  11.3 1.7 %slice_subtract_fusion.5 = f32[31,32,512]{2,1,0:T(8,128)} fusion(f32[32,32,512]{2,1,0:T(8,128)S(1)} %copy-done), kind=kLoop, calls=%fused_computation.46 | loop fusion | flops 507904 | bytes 6094848 | tf_op jit(solution)/shard_map/sub | solution.py:48
  13.1 4.5 %fusion.1 = (f32[32,32,512]{2,1,0:T(8,128)S(1)}, f32[32,32,512]{2,1,0:T(8,128)S(1)}, f32[32,32,512]{2,1,0:T(8,128)S(1)}) fusion(f32[32,32,512]{2,1,0:T(8,128)} %param.3, f32[1,32,512]{2,1,0:T(8,128)S(1)} %subtract_multiply_fusion.1, f32[31,32,512]{2,1,0:T(8,128)} %slice_subtract_fusion.5, f32[32,32,511]{2,1,0:T(8,128)} %slice_subtract_fusion.2, ...), kind=kLoop, calls=%fused_computation.5 | loop fusion | flops 6291456 | bytes 14675968 | tf_op jit(solution)/shard_map/jit(clip)/min | solution.py:53
  17.7 3.0 %collective-permute-start.3 = (f32[32,1,512]{2,1,0:T(1,128)S(1)}, f32[32,1,512]{2,1,0:T(1,128)S(1)}, u32[]{:S(2)}, u32[]{:S(2)}) collective-permute-start(f32[32,1,512]{2,1,0:T(1,128)S(1)} %slice.122), channel_id=1, source_target_pairs={{0,1},{1,2},{2,3},{3,4},{4,5},{5,6},{6,7},{8,9},{9,10},{10,11},{11... | collective-permute-start | bytes 196616 | tf_op jit(solution)/shard_map/ppermute | solution.py:14
  20.8 5.6 %collective-permute-start.1 = (f32[1,32,512]{2,1,0:T(8,128)S(1)}, f32[1,32,512]{2,1,0:T(8,128)S(1)}, u32[]{:S(2)}, u32[]{:S(2)}) collective-permute-start(f32[1,32,512]{2,1,0:T(8,128)S(1)} %slice.120), channel_id=1, source_target_pairs={{0,8},{8,16},{16,24},{1,9},{9,17},{17,25},{2,10},{10,18},{18,26},{... | collective-permute-start | bytes 196616 | tf_op jit(solution)/shard_map/ppermute | solution.py:14
  26.6 1.6 %collective-permute-done.1 = f32[1,32,512]{2,1,0:T(8,128)S(1)} collective-permute-done((f32[1,32,512]{2,1,0:T(8,128)S(1)}, f32[1,32,512]{2,1,0:T(8,128)S(1)}, u32[]{:S(2)}, u32[]{:S(2)}) %collective-permute-start.1) | collective-permute-done | bytes 65568 | tf_op jit(solution)/shard_map/ppermute | solution.py:14
  28.3 3.5 %multiply_subtract_fusion = (f32[32,32,512]{2,1,0:T(8,128)S(1)}, f32[32,32,512]{2,1,0:T(8,128)}) fusion(f32[32,32,512]{2,1,0:T(8,128)S(1)} %copy-done, f32[32,32,512]{2,1,0:T(8,128)S(1)} %get-tuple-element.24, f32[32,32,511]{2,1,0:T(8,128)S(1)} %bitcast.18, f32[32,32,512]{2,1,0:T(8,128)S(1)} %get-tuple-element.25, f32[32,31,512]{2,1,0:T(8,128)S(1)} %bitcast.15, ...), kind=kLoop, calls=%fused_computation.41 | loop fusion | flops 6815744 | bytes 18870272 | tf_op jit(solution)/shard_map/sub | solution.py:69
  32.1 0.6 slice_subtract_fusion
  32.7 1.4 %collective-permute-start.4 = (f32[1,32,512]{2,1,0:T(8,128)S(1)}, f32[1,32,512]{2,1,0:T(8,128)S(1)}, u32[]{:S(2)}, u32[]{:S(2)}) collective-permute-start(f32[1,32,512]{2,1,0:T(8,128)S(1)} %slice.127), channel_id=1, source_target_pairs={{8,0},{16,8},{24,16},{9,1},{17,9},{25,17},{10,2},{18,10},{26,18},{... | collective-permute-start | bytes 196616 | tf_op jit(solution)/shard_map/ppermute | solution.py:14
  34.4 1.3 %collective-permute-start.6 = (f32[32,1,512]{2,1,0:T(1,128)S(1)}, f32[32,1,512]{2,1,0:T(1,128)S(1)}, u32[]{:S(2)}, u32[]{:S(2)}) collective-permute-start(f32[32,1,512]{2,1,0:T(1,128)S(1)} %slice.133), channel_id=1, source_target_pairs={{1,0},{2,1},{3,2},{4,3},{5,4},{6,5},{7,6},{9,8},{10,9},{11,10},{12... | collective-permute-start | bytes 196616 | tf_op jit(solution)/shard_map/ppermute | solution.py:14
  35.7 4.2 %collective-permute-done.4 = f32[1,32,512]{2,1,0:T(8,128)S(1)} collective-permute-done((f32[1,32,512]{2,1,0:T(8,128)S(1)}, f32[1,32,512]{2,1,0:T(8,128)S(1)}, u32[]{:S(2)}, u32[]{:S(2)}) %collective-permute-start.4) | collective-permute-done | bytes 65568 | tf_op jit(solution)/shard_map/ppermute | solution.py:14
  40.0 3.8 %multiply_reduce_fusion.6 = (f32[]{:T(128)}, f32[]{:T(128)}, f32[32,32,512]{2,1,0:T(8,128)S(1)}, f32[]{:T(128)}, f32[32,32,512]{2,1,0:T(8,128)}, /*index=5*/f32[...) fusion(f32[32,32,512]{2,1,0:T(8,128)S(1)} %get-tuple-element.23, f32[32,32,512]{2,1,0:T(8,128)S(1)} %copy-done.6, ...), kind=kLoop, calls=%fused_computation.38 | loop fusion | flops 15728634 | bytes 20967448 | tf_op jit(solution)/shard_map/reduce_sum | solution.py:64
  43.9 2.7 %collective-permute-start.7 = (f32[32,1,512]{2,1,0:T(1,128)S(1)}, f32[32,1,512]{2,1,0:T(1,128)S(1)}, u32[]{:S(2)}, u32[]{:S(2)}) collective-permute-start(f32[32,1,512]{2,1,0:T(1,128)S(1)} %slice.135), channel_id=1, source_target_pairs={{0,1},{1,2},{2,3},{3,4},{4,5},{5,6},{6,7},{8,9},{9,10},{10,11},{11... | collective-permute-start | bytes 196616 | tf_op jit(solution)/shard_map/ppermute | solution.py:14
  46.6 4.7 %collective-permute-start.5 = (f32[1,32,512]{2,1,0:T(8,128)S(1)}, f32[1,32,512]{2,1,0:T(8,128)S(1)}, u32[]{:S(2)}, u32[]{:S(2)}) collective-permute-start(f32[1,32,512]{2,1,0:T(8,128)S(1)} %slice.129), channel_id=1, source_target_pairs={{0,8},{8,16},{16,24},{1,9},{9,17},{17,25},{2,10},{10,18},{18,26},{... | collective-permute-start | bytes 196616 | tf_op jit(solution)/shard_map/ppermute | solution.py:14
  51.4 1.5 %slice.130 = f32[31,32,512]{2,1,0:T(8,128)} slice(f32[32,32,512]{2,1,0:T(8,128)S(1)} %get-tuple-element.14), slice={[0:31], [0:32], [0:512]} | slice | bytes 4063232 | tf_op jit(solution)/shard_map/slice | solution.py:58
  56.7 8.3 %multiply_reduce_fusion.7 = (f32[]{:T(128)}, f32[]{:T(128)}, f32[32,32,512]{2,1,0:T(8,128)}) fusion(f32[32,32,512]{2,1,0:T(8,128)S(1)} %copy-done, f32[32,32,512]{2,1,0:T(8,128)} %get-tuple-element.16, f32[32,32,512]{2,1,0:T(8,128)} %get-tuple-element.18, f32[32,32,511]{2,1,0:T(8,128)} %bitcast.19, f32[32,32,512]{2,1,0:T(8,128)} %copy-done.1, ...), kind=kLoop, calls=%fused_computation.39 | loop fusion | flops 9961470 | bytes 18870280 | tf_op jit(solution)/shard_map/reduce_sum | solution.py:62
  65.0 1.4 %maximum_bitcast_fusion = (f32[1,2]{1,0:T(1,128)S(1)}, f32[1,2]{1,0:T(1,128)S(1)}) fusion(f32[1]{0:T(128)} %bitcast.4, f32[1]{0:T(128)} %bitcast.3, f32[1]{0:T(128)} %bitcast.7, f32[1]{0:T(128)} %bitcast.6), kind=kLoop, calls=%fused_computation.54 | loop fusion | flops 4 | bytes 32 | tf_op jit(solution)/shard_map/stack | solution.py:28
  66.4 3.4 %pad_maximum_fusion = f32[3,32,32,512]{3,2,1,0:T(8,128)} fusion(f32[1,32,32,512]{3,2,1,0:T(8,128)S(1)} %bitcast.20, f32[1,32,32,512]{3,2,1,0:T(8,128)S(1)} %bitcast.17, f32[1,32,32,512]{3,2,1,0:T(8,128)S(1)} %bitcast.21), kind=kLoop, calls=%fused_computation | loop fusion | flops 3145728 | bytes 12582912 | tf_op jit(solution)/shard_map/stack | solution.py:73
  69.8 40.5 %psum.7 = f32[2,2]{1,0:T(2,128)S(1)} all-reduce(f32[2,2]{1,0:T(2,128)S(1)} %pad_maximum_fusion.1), channel_id=1, replica_groups=mesh['inl'=4,'xln'=8] {'inl','xln'}, use_global_device_ids=true, to_apply=%region_8.9 | all-reduce | flops 4 | bytes 32 | tf_op jit(solution)/shard_map/psum | solution.py:28
  (35 shorter events, 1.8 us)
Async XLA Ops:
  1.5 11.5 %collective-permute-start = (f32[1,32,512]{2,1,0:T(8,128)S(1)}, f32[1,32,512]{2,1,0:T(8,128)S(1)}, u32[]{:S(2)}, u32[]{:S(2)}) collective-permute-start(f32[1,32,512]{2,1,0:T(8,128)S(1)} %slice.92), channel_id=1, source_target_pairs={{8,0},{16,8},{24,16},{9,1},{17,9},{25,17},{10,2},{18,10},{26,18},{... | collective-permute-start | bytes 196616 | tf_op jit(solution)/shard_map/ppermute | solution.py:14
  3.8 5.5 %copy-start = (f32[32,32,512]{2,1,0:T(8,128)S(1)}, f32[32,32,512]{2,1,0:T(8,128)}, u32[]{:S(2)}) copy-start(f32[32,32,512]{2,1,0:T(8,128)} %param.2) | copy-start | bytes 6291460
  3.9 9.2 %collective-permute-start.2 = (f32[32,1,512]{2,1,0:T(1,128)S(1)}, f32[32,1,512]{2,1,0:T(1,128)S(1)}, u32[]{:S(2)}, u32[]{:S(2)}) collective-permute-start(f32[32,1,512]{2,1,0:T(1,128)S(1)} %slice.98), channel_id=1, source_target_pairs={{1,0},{2,1},{3,2},{4,3},{5,4},{6,5},{7,6},{9,8},{10,9},{11,10},{12... | collective-permute-start | bytes 196616 | tf_op jit(solution)/shard_map/ppermute | solution.py:14
  17.7 8.9 %collective-permute-start.3 = (f32[32,1,512]{2,1,0:T(1,128)S(1)}, f32[32,1,512]{2,1,0:T(1,128)S(1)}, u32[]{:S(2)}, u32[]{:S(2)}) collective-permute-start(f32[32,1,512]{2,1,0:T(1,128)S(1)} %slice.122), channel_id=1, source_target_pairs={{0,1},{1,2},{2,3},{3,4},{4,5},{5,6},{6,7},{8,9},{9,10},{10,11},{11... | collective-permute-start | bytes 196616 | tf_op jit(solution)/shard_map/ppermute | solution.py:14
  20.8 7.5 %collective-permute-start.1 = (f32[1,32,512]{2,1,0:T(8,128)S(1)}, f32[1,32,512]{2,1,0:T(8,128)S(1)}, u32[]{:S(2)}, u32[]{:S(2)}) collective-permute-start(f32[1,32,512]{2,1,0:T(8,128)S(1)} %slice.120), channel_id=1, source_target_pairs={{0,8},{8,16},{16,24},{1,9},{9,17},{17,25},{2,10},{10,18},{18,26},{... | collective-permute-start | bytes 196616 | tf_op jit(solution)/shard_map/ppermute | solution.py:14
  32.7 7.3 %copy-start.6 = (f32[32,32,512]{2,1,0:T(8,128)S(1)}, f32[32,32,512]{2,1,0:T(8,128)}, u32[]{:S(2)}) copy-start(f32[32,32,512]{2,1,0:T(8,128)} %param.3) | copy-start | bytes 6291460
  32.7 7.2 %collective-permute-start.4 = (f32[1,32,512]{2,1,0:T(8,128)S(1)}, f32[1,32,512]{2,1,0:T(8,128)S(1)}, u32[]{:S(2)}, u32[]{:S(2)}) collective-permute-start(f32[1,32,512]{2,1,0:T(8,128)S(1)} %slice.127), channel_id=1, source_target_pairs={{8,0},{16,8},{24,16},{9,1},{17,9},{25,17},{10,2},{18,10},{26,18},{... | collective-permute-start | bytes 196616 | tf_op jit(solution)/shard_map/ppermute | solution.py:14
  34.4 5.5 %collective-permute-start.6 = (f32[32,1,512]{2,1,0:T(1,128)S(1)}, f32[32,1,512]{2,1,0:T(1,128)S(1)}, u32[]{:S(2)}, u32[]{:S(2)}) collective-permute-start(f32[32,1,512]{2,1,0:T(1,128)S(1)} %slice.133), channel_id=1, source_target_pairs={{1,0},{2,1},{3,2},{4,3},{5,4},{6,5},{7,6},{9,8},{10,9},{11,10},{12... | collective-permute-start | bytes 196616 | tf_op jit(solution)/shard_map/ppermute | solution.py:14
  43.8 9.1 %copy-start.1 = (f32[32,32,512]{2,1,0:T(8,128)}, f32[32,32,512]{2,1,0:T(8,128)S(1)}, u32[]{:S(2)}) copy-start(f32[32,32,512]{2,1,0:T(8,128)S(1)} %get-tuple-element.21) | copy-start | bytes 6291460
  43.8 9.1 %copy-start.4 = (f32[32,32,512]{2,1,0:T(8,128)}, f32[32,32,512]{2,1,0:T(8,128)S(1)}, u32[]{:S(2)}) copy-start(f32[32,32,512]{2,1,0:T(8,128)S(1)} %get-tuple-element.14) | copy-start | bytes 6291460
  43.9 12.7 %collective-permute-start.7 = (f32[32,1,512]{2,1,0:T(1,128)S(1)}, f32[32,1,512]{2,1,0:T(1,128)S(1)}, u32[]{:S(2)}, u32[]{:S(2)}) collective-permute-start(f32[32,1,512]{2,1,0:T(1,128)S(1)} %slice.135), channel_id=1, source_target_pairs={{0,1},{1,2},{2,3},{3,4},{4,5},{5,6},{6,7},{8,9},{9,10},{10,11},{11... | collective-permute-start | bytes 196616 | tf_op jit(solution)/shard_map/ppermute | solution.py:14
  46.6 10.0 %collective-permute-start.5 = (f32[1,32,512]{2,1,0:T(8,128)S(1)}, f32[1,32,512]{2,1,0:T(8,128)S(1)}, u32[]{:S(2)}, u32[]{:S(2)}) collective-permute-start(f32[1,32,512]{2,1,0:T(8,128)S(1)} %slice.129), channel_id=1, source_target_pairs={{0,8},{8,16},{16,24},{1,9},{9,17},{17,25},{2,10},{10,18},{18,26},{... | collective-permute-start | bytes 196616 | tf_op jit(solution)/shard_map/ppermute | solution.py:14
  56.7 9.7 %copy-start.2 = (f32[32,32,512]{2,1,0:T(8,128)S(1)}, f32[32,32,512]{2,1,0:T(8,128)}, u32[]{:S(2)}) copy-start(f32[32,32,512]{2,1,0:T(8,128)} %copy-done.1) | copy-start | bytes 6291460
  56.7 9.7 %copy-start.3 = (f32[32,32,512]{2,1,0:T(8,128)S(1)}, f32[32,32,512]{2,1,0:T(8,128)}, u32[]{:S(2)}) copy-start(f32[32,32,512]{2,1,0:T(8,128)} %get-tuple-element.18) | copy-start | bytes 6291460
  56.7 9.7 %copy-start.5 = (f32[32,32,512]{2,1,0:T(8,128)S(1)}, f32[32,32,512]{2,1,0:T(8,128)}, u32[]{:S(2)}) copy-start(f32[32,32,512]{2,1,0:T(8,128)} %copy-done.4) | copy-start | bytes 6291460
where the time goes:
time: 111 us
  blocking collectives  40.5 us (36%)
  other arithmetic  33.9 us (31%)
  starting transfers between devices  21.5 us (19%)
  waiting for transfers between devices  5.79 us (5%)
  between operations  4.65 us (4%)
  local copies, waits for them, and re-layouts  4.5 us (4%)
    psum x1, blocking collectives, finish(): return jnp.sqrt(lax.psum(jnp.stack(sums_list), ('inl', 'xln')))  40.5 us
    ppermute x8, starting transfers between devices, passed_along(): lax.ppermute(value, axis, [(source, source + steps) for source in range(f...  21.5 us
    reduce_sum x1, other arithmetic, per_device(): primal_sum = jnp.sum((updated - primal) ** 2)  8.26 us
    ppermute x8, waiting for transfers between devices, passed_along(): lax.ppermute(value, axis, [(source, source + steps) for source in range(f...  5.79 us
    min x1, other arithmetic, per_device(): fresh_i = jnp.clip(dual_i + SIGMA * grad_i, -bound, bound)  4.53 us
    sub x2, other arithmetic, per_device(): smooth[:, 1:] - smooth[:, :-1]  4.4 us
    reduce_sum x1, other arithmetic, per_device(): jnp.sum((fresh_i - dual_i) ** 2) + jnp.sum((fresh_x - dual_x) ** 2)  3.83 us
    sub x1, other arithmetic, per_device(): smooth = 2.0 * updated - primal  3.47 us
  transfers between devices with their start and end apart: 8, of which 2 were waited for; matrix products, arithmetic and copies ran while one was open for 10% of the time, Pallas kernels for 0%

commit v1 on v0

--- a/solution.py
+++ b/solution.py
@@ -25,7 +25,10 @@
 
 
 def finish(sums_list):
-    return jnp.sqrt(lax.psum(jnp.stack(sums_list), ("inl", "xln")))
+    settle_halves_up = lambda my_tile, bus_axis, which_axis: lax.psum(
+        lax.psum(my_tile, axis_name=bus_axis), axis_name=which_axis
+    )
+    return jnp.sqrt(settle_halves_up(jnp.stack(sums_list), "xln", "inl"))
 
 
 def record(primal_sum, dual_sum, sums_list):

time: 111 us -> 96.8 us (0.87)
  blocking collectives: 40.5 us -> 22.3 us
  other arithmetic: 33.9 us -> 37.4 us
    psum x1 -> x2, blocking collectives: 40.5 us -> 22.3 us  [the longest x1 11.8 us: finish(): lax.psum(my_tile, axis_name=bus_axis)]
    another operation x1, other arithmetic: 3.41 us -> 6.89 us  [per_device(): return (primal, jnp.stack([dual_i, dual_x, dual_z]), norms)]
  transfers between devices with their start and end apart: 8 -> 8, of which waited for: 2 -> 2; matrix products, arithmetic and copies ran while one was open for 10% -> 11% of each run, Pallas kernels for 0% -> 0%
where the time goes in v1:
time: 96.8 us; the launch traced here: 96 us
  other arithmetic  37.4 us (39%)
  blocking collectives  22.3 us (23%)
  starting transfers between devices  21.5 us (22%)
  waiting for transfers between devices  5.79 us (6%)
  between operations  4.55 us (5%)
  local copies, waits for them, and re-layouts  4.46 us (5%)
    ppermute x8, starting transfers between devices, passed_along(): lax.ppermute(value, axis, [(source, source + steps) for source in range(f...  21.5 us
    psum x1, blocking collectives, finish(): lax.psum(my_tile, axis_name=bus_axis)  11.8 us
    psum x1, blocking collectives, finish(): lax.psum(lax.psum(my_tile, axis_name=bus_axis), axis_name=which_axis)  10.5 us
    reduce_sum x1, other arithmetic, per_device(): primal_sum = jnp.sum((updated - primal) ** 2)  8.23 us
    another operation x1, other arithmetic, per_device(): return (primal, jnp.stack([dual_i, dual_x, dual_z]), norms)  6.89 us
    ppermute x8, waiting for transfers between devices, passed_along(): lax.ppermute(value, axis, [(source, source + steps) for source in range(f...  5.79 us
    min x1, other arithmetic, per_device(): fresh_i = jnp.clip(dual_i + SIGMA * grad_i, -bound, bound)  4.53 us
    sub x2, other arithmetic, per_device(): smooth[:, 1:] - smooth[:, :-1]  4.4 us
  transfers between devices with their start and end apart: 8, of which 2 were waited for; matrix products, arithmetic and copies ran while one was open for 11% of the time, Pallas kernels for 0%

profile of v1, /device:TPU:0, one launch (start us, length us, event | category | flops | bytes accessed | tf_op | source)
XLA Modules:
  0.0 96.0 jit_solution(15639891389835570270)
XLA Ops:
  0.6 0.8 slice.92
  1.5 1.3 %collective-permute-start = (f32[1,32,512]{2,1,0:T(8,128)S(1)}, f32[1,32,512]{2,1,0:T(8,128)S(1)}, u32[]{:S(2)}, u32[]{:S(2)}) collective-permute-start(f32[1,32,512]{2,1,0:T(8,128)S(1)} %slice.92), channel_id=1, source_target_pairs={{8,0},{16,8},{24,16},{9,1},{17,9},{25,17},{10,2},{18,10},{26,18},{... | collective-permute-start | bytes 196616 | tf_op jit(solution)/shard_map/ppermute | solution.py:14
  2.8 1.1 %slice.98 = f32[32,1,512]{2,1,0:T(1,128)S(1)} slice(f32[32,32,512]{2,1,0:T(8,128)} %param.2), slice={[0:32], [0:1], [0:512]} | slice | bytes 131072 | tf_op jit(solution)/shard_map/slice | solution.py:49
  3.9 1.4 %collective-permute-start.2 = (f32[32,1,512]{2,1,0:T(1,128)S(1)}, f32[32,1,512]{2,1,0:T(1,128)S(1)}, u32[]{:S(2)}, u32[]{:S(2)}) collective-permute-start(f32[32,1,512]{2,1,0:T(1,128)S(1)} %slice.98), channel_id=1, source_target_pairs={{1,0},{2,1},{3,2},{4,3},{5,4},{6,5},{7,6},{9,8},{10,9},{11,10},{12... | collective-permute-start | bytes 196616 | tf_op jit(solution)/shard_map/ppermute | solution.py:14
  5.3 4.1 %slice_subtract_fusion.3 = f32[32,31,512]{2,1,0:T(8,128)} fusion(f32[32,32,512]{2,1,0:T(8,128)} %param.2), kind=kLoop, calls=%fused_computation.44 | loop fusion | flops 507904 | bytes 6094848 | tf_op jit(solution)/shard_map/sub | solution.py:54
  9.4 2.0 %slice_subtract_fusion.2 = f32[32,32,511]{2,1,0:T(8,128)} fusion(f32[32,32,512]{2,1,0:T(8,128)S(1)} %copy-done), kind=kLoop, calls=%fused_computation.43 | loop fusion | flops 523264 | bytes 6279168 | tf_op jit(solution)/shard_map/sub | solution.py:19
  11.3 1.7 %slice_subtract_fusion.5 = f32[31,32,512]{2,1,0:T(8,128)} fusion(f32[32,32,512]{2,1,0:T(8,128)S(1)} %copy-done), kind=kLoop, calls=%fused_computation.46 | loop fusion | flops 507904 | bytes 6094848 | tf_op jit(solution)/shard_map/sub | solution.py:51
  13.1 4.5 %fusion.1 = (f32[32,32,512]{2,1,0:T(8,128)S(1)}, f32[32,32,512]{2,1,0:T(8,128)S(1)}, f32[32,32,512]{2,1,0:T(8,128)S(1)}) fusion(f32[32,32,512]{2,1,0:T(8,128)} %param.3, f32[1,32,512]{2,1,0:T(8,128)S(1)} %subtract_multiply_fusion.1, f32[31,32,512]{2,1,0:T(8,128)} %slice_subtract_fusion.5, f32[32,32,511]{2,1,0:T(8,128)} %slice_subtract_fusion.2, ...), kind=kLoop, calls=%fused_computation.5 | loop fusion | flops 6291456 | bytes 14675968 | tf_op jit(solution)/shard_map/jit(clip)/min | solution.py:56
  17.7 3.0 %collective-permute-start.3 = (f32[32,1,512]{2,1,0:T(1,128)S(1)}, f32[32,1,512]{2,1,0:T(1,128)S(1)}, u32[]{:S(2)}, u32[]{:S(2)}) collective-permute-start(f32[32,1,512]{2,1,0:T(1,128)S(1)} %slice.122), channel_id=1, source_target_pairs={{0,1},{1,2},{2,3},{3,4},{4,5},{5,6},{6,7},{8,9},{9,10},{10,11},{11... | collective-permute-start | bytes 196616 | tf_op jit(solution)/shard_map/ppermute | solution.py:14
  20.8 5.6 %collective-permute-start.1 = (f32[1,32,512]{2,1,0:T(8,128)S(1)}, f32[1,32,512]{2,1,0:T(8,128)S(1)}, u32[]{:S(2)}, u32[]{:S(2)}) collective-permute-start(f32[1,32,512]{2,1,0:T(8,128)S(1)} %slice.120), channel_id=1, source_target_pairs={{0,8},{8,16},{16,24},{1,9},{9,17},{17,25},{2,10},{10,18},{18,26},{... | collective-permute-start | bytes 196616 | tf_op jit(solution)/shard_map/ppermute | solution.py:14
  26.6 1.6 %collective-permute-done.1 = f32[1,32,512]{2,1,0:T(8,128)S(1)} collective-permute-done((f32[1,32,512]{2,1,0:T(8,128)S(1)}, f32[1,32,512]{2,1,0:T(8,128)S(1)}, u32[]{:S(2)}, u32[]{:S(2)}) %collective-permute-start.1) | collective-permute-done | bytes 65568 | tf_op jit(solution)/shard_map/ppermute | solution.py:14
  28.3 3.5 %multiply_subtract_fusion = (f32[32,32,512]{2,1,0:T(8,128)S(1)}, f32[32,32,512]{2,1,0:T(8,128)}) fusion(f32[32,32,512]{2,1,0:T(8,128)S(1)} %copy-done, f32[32,32,512]{2,1,0:T(8,128)S(1)} %get-tuple-element.24, f32[32,32,511]{2,1,0:T(8,128)S(1)} %bitcast.18, f32[32,32,512]{2,1,0:T(8,128)S(1)} %get-tuple-element.25, f32[32,31,512]{2,1,0:T(8,128)S(1)} %bitcast.15, ...), kind=kLoop, calls=%fused_computation.41 | loop fusion | flops 6815744 | bytes 18870272 | tf_op jit(solution)/shard_map/sub | solution.py:72
  32.7 1.4 %collective-permute-start.4 = (f32[1,32,512]{2,1,0:T(8,128)S(1)}, f32[1,32,512]{2,1,0:T(8,128)S(1)}, u32[]{:S(2)}, u32[]{:S(2)}) collective-permute-start(f32[1,32,512]{2,1,0:T(8,128)S(1)} %slice.127), channel_id=1, source_target_pairs={{8,0},{16,8},{24,16},{9,1},{17,9},{25,17},{10,2},{18,10},{26,18},{... | collective-permute-start | bytes 196616 | tf_op jit(solution)/shard_map/ppermute | solution.py:14
  34.4 1.3 %collective-permute-start.6 = (f32[32,1,512]{2,1,0:T(1,128)S(1)}, f32[32,1,512]{2,1,0:T(1,128)S(1)}, u32[]{:S(2)}, u32[]{:S(2)}) collective-permute-start(f32[32,1,512]{2,1,0:T(1,128)S(1)} %slice.133), channel_id=1, source_target_pairs={{1,0},{2,1},{3,2},{4,3},{5,4},{6,5},{7,6},{9,8},{10,9},{11,10},{12... | collective-permute-start | bytes 196616 | tf_op jit(solution)/shard_map/ppermute | solution.py:14
  35.7 4.2 %collective-permute-done.4 = f32[1,32,512]{2,1,0:T(8,128)S(1)} collective-permute-done((f32[1,32,512]{2,1,0:T(8,128)S(1)}, f32[1,32,512]{2,1,0:T(8,128)S(1)}, u32[]{:S(2)}, u32[]{:S(2)}) %collective-permute-start.4) | collective-permute-done | bytes 65568 | tf_op jit(solution)/shard_map/ppermute | solution.py:14
  40.0 3.9 %multiply_reduce_fusion.6 = (f32[]{:T(128)}, f32[]{:T(128)}, f32[32,32,512]{2,1,0:T(8,128)S(1)}, f32[]{:T(128)}, f32[32,32,512]{2,1,0:T(8,128)}, /*index=5*/f32[...) fusion(f32[32,32,512]{2,1,0:T(8,128)S(1)} %get-tuple-element.23, f32[32,32,512]{2,1,0:T(8,128)S(1)} %copy-done.3, ...), kind=kLoop, calls=%fused_computation.38 | loop fusion | flops 15728634 | bytes 20967448 | tf_op jit(solution)/shard_map/reduce_sum | solution.py:67
  44.0 2.7 %collective-permute-start.7 = (f32[32,1,512]{2,1,0:T(1,128)S(1)}, f32[32,1,512]{2,1,0:T(1,128)S(1)}, u32[]{:S(2)}, u32[]{:S(2)}) collective-permute-start(f32[32,1,512]{2,1,0:T(1,128)S(1)} %slice.135), channel_id=1, source_target_pairs={{0,1},{1,2},{2,3},{3,4},{4,5},{5,6},{6,7},{8,9},{9,10},{10,11},{11... | collective-permute-start | bytes 196616 | tf_op jit(solution)/shard_map/ppermute | solution.py:14
  46.7 4.7 %collective-permute-start.5 = (f32[1,32,512]{2,1,0:T(8,128)S(1)}, f32[1,32,512]{2,1,0:T(8,128)S(1)}, u32[]{:S(2)}, u32[]{:S(2)}) collective-permute-start(f32[1,32,512]{2,1,0:T(8,128)S(1)} %slice.129), channel_id=1, source_target_pairs={{0,8},{8,16},{16,24},{1,9},{9,17},{17,25},{2,10},{10,18},{18,26},{... | collective-permute-start | bytes 196616 | tf_op jit(solution)/shard_map/ppermute | solution.py:14
  51.4 1.5 %slice.130 = f32[31,32,512]{2,1,0:T(8,128)} slice(f32[32,32,512]{2,1,0:T(8,128)S(1)} %get-tuple-element.14), slice={[0:31], [0:32], [0:512]} | slice | bytes 4063232 | tf_op jit(solution)/shard_map/slice | solution.py:61
  56.7 8.2 %multiply_reduce_fusion.7 = (f32[]{:T(128)}, f32[]{:T(128)}, f32[32,32,512]{2,1,0:T(8,128)}) fusion(f32[32,32,512]{2,1,0:T(8,128)S(1)} %copy-done, f32[32,32,512]{2,1,0:T(8,128)} %get-tuple-element.16, f32[32,32,512]{2,1,0:T(8,128)} %get-tuple-element.18, f32[32,32,511]{2,1,0:T(8,128)} %bitcast.19, f32[32,32,512]{2,1,0:T(8,128)} %copy-done.1, ...), kind=kLoop, calls=%fused_computation.39 | loop fusion | flops 9961470 | bytes 18870280 | tf_op jit(solution)/shard_map/reduce_sum | solution.py:65
  64.9 1.3 %maximum_bitcast_fusion = (f32[1,2]{1,0:T(1,128)S(1)}, f32[1,2]{1,0:T(1,128)S(1)}) fusion(f32[1]{0:T(128)} %bitcast.4, f32[1]{0:T(128)} %bitcast.3, f32[1]{0:T(128)} %bitcast.7, f32[1]{0:T(128)} %bitcast.6), kind=kLoop, calls=%fused_computation.54 | loop fusion | flops 4 | bytes 32 | tf_op jit(solution)/shard_map/stack | solution.py:31
  66.2 11.8 %psum.14 = f32[2,2]{1,0:T(2,128)S(1)} all-reduce(f32[2,2]{1,0:T(2,128)S(1)} %pad_maximum_fusion.1), channel_id=1, replica_groups=mesh['inl'=4,'xln'=8] {'xln'}, use_global_device_ids=true, to_apply=%region_8.9 | all-reduce | flops 4 | bytes 32 | tf_op jit(solution)/shard_map/psum | solution.py:29
  78.0 6.9 %pad_maximum_fusion = f32[3,32,32,512]{3,2,1,0:T(8,128)} fusion(f32[1,32,32,512]{3,2,1,0:T(8,128)} %bitcast.20, f32[1,32,32,512]{3,2,1,0:T(8,128)} %bitcast.17, f32[1,32,32,512]{3,2,1,0:T(8,128)} %bitcast.21), kind=kLoop, calls=%fused_computation | loop fusion | flops 3145728 | bytes 12582912 | tf_op jit(solution)/shard_map/stack | solution.py:76
  84.9 10.5 %psum.15 = f32[2,2]{1,0:T(2,128)S(1)} all-reduce(f32[2,2]{1,0:T(2,128)S(1)} %psum.14), channel_id=1, replica_groups=mesh['inl'=4,'xln'=8] {'inl'}, use_global_device_ids=true, to_apply=%region_9.10 | all-reduce | flops 4 | bytes 32 | tf_op jit(solution)/shard_map/psum | solution.py:28
  (30 shorter events, 2.4 us)
Async XLA Ops:
  1.5 11.5 %collective-permute-start = (f32[1,32,512]{2,1,0:T(8,128)S(1)}, f32[1,32,512]{2,1,0:T(8,128)S(1)}, u32[]{:S(2)}, u32[]{:S(2)}) collective-permute-start(f32[1,32,512]{2,1,0:T(8,128)S(1)} %slice.92), channel_id=1, source_target_pairs={{8,0},{16,8},{24,16},{9,1},{17,9},{25,17},{10,2},{18,10},{26,18},{... | collective-permute-start | bytes 196616 | tf_op jit(solution)/shard_map/ppermute | solution.py:14
  3.8 5.5 %copy-start = (f32[32,32,512]{2,1,0:T(8,128)S(1)}, f32[32,32,512]{2,1,0:T(8,128)}, u32[]{:S(2)}) copy-start(f32[32,32,512]{2,1,0:T(8,128)} %param.2) | copy-start | bytes 6291460
  3.9 9.2 %collective-permute-start.2 = (f32[32,1,512]{2,1,0:T(1,128)S(1)}, f32[32,1,512]{2,1,0:T(1,128)S(1)}, u32[]{:S(2)}, u32[]{:S(2)}) collective-permute-start(f32[32,1,512]{2,1,0:T(1,128)S(1)} %slice.98), channel_id=1, source_target_pairs={{1,0},{2,1},{3,2},{4,3},{5,4},{6,5},{7,6},{9,8},{10,9},{11,10},{12... | collective-permute-start | bytes 196616 | tf_op jit(solution)/shard_map/ppermute | solution.py:14
  17.7 8.9 %collective-permute-start.3 = (f32[32,1,512]{2,1,0:T(1,128)S(1)}, f32[32,1,512]{2,1,0:T(1,128)S(1)}, u32[]{:S(2)}, u32[]{:S(2)}) collective-permute-start(f32[32,1,512]{2,1,0:T(1,128)S(1)} %slice.122), channel_id=1, source_target_pairs={{0,1},{1,2},{2,3},{3,4},{4,5},{5,6},{6,7},{8,9},{9,10},{10,11},{11... | collective-permute-start | bytes 196616 | tf_op jit(solution)/shard_map/ppermute | solution.py:14
  20.8 7.5 %collective-permute-start.1 = (f32[1,32,512]{2,1,0:T(8,128)S(1)}, f32[1,32,512]{2,1,0:T(8,128)S(1)}, u32[]{:S(2)}, u32[]{:S(2)}) collective-permute-start(f32[1,32,512]{2,1,0:T(8,128)S(1)} %slice.120), channel_id=1, source_target_pairs={{0,8},{8,16},{16,24},{1,9},{9,17},{17,25},{2,10},{10,18},{18,26},{... | collective-permute-start | bytes 196616 | tf_op jit(solution)/shard_map/ppermute | solution.py:14
  32.7 7.3 %copy-start.3 = (f32[32,32,512]{2,1,0:T(8,128)S(1)}, f32[32,32,512]{2,1,0:T(8,128)}, u32[]{:S(2)}) copy-start(f32[32,32,512]{2,1,0:T(8,128)} %param.3) | copy-start | bytes 6291460
  32.7 7.2 %collective-permute-start.4 = (f32[1,32,512]{2,1,0:T(8,128)S(1)}, f32[1,32,512]{2,1,0:T(8,128)S(1)}, u32[]{:S(2)}, u32[]{:S(2)}) collective-permute-start(f32[1,32,512]{2,1,0:T(8,128)S(1)} %slice.127), channel_id=1, source_target_pairs={{8,0},{16,8},{24,16},{9,1},{17,9},{25,17},{10,2},{18,10},{26,18},{... | collective-permute-start | bytes 196616 | tf_op jit(solution)/shard_map/ppermute | solution.py:14
  34.4 5.5 %collective-permute-start.6 = (f32[32,1,512]{2,1,0:T(1,128)S(1)}, f32[32,1,512]{2,1,0:T(1,128)S(1)}, u32[]{:S(2)}, u32[]{:S(2)}) collective-permute-start(f32[32,1,512]{2,1,0:T(1,128)S(1)} %slice.133), channel_id=1, source_target_pairs={{1,0},{2,1},{3,2},{4,3},{5,4},{6,5},{7,6},{9,8},{10,9},{11,10},{12... | collective-permute-start | bytes 196616 | tf_op jit(solution)/shard_map/ppermute | solution.py:14
  43.9 9.0 %copy-start.1 = (f32[32,32,512]{2,1,0:T(8,128)}, f32[32,32,512]{2,1,0:T(8,128)S(1)}, u32[]{:S(2)}) copy-start(f32[32,32,512]{2,1,0:T(8,128)S(1)} %get-tuple-element.21) | copy-start | bytes 6291460
  43.9 9.0 %copy-start.2 = (f32[32,32,512]{2,1,0:T(8,128)}, f32[32,32,512]{2,1,0:T(8,128)S(1)}, u32[]{:S(2)}) copy-start(f32[32,32,512]{2,1,0:T(8,128)S(1)} %get-tuple-element.14) | copy-start | bytes 6291460
  44.0 12.7 %collective-permute-start.7 = (f32[32,1,512]{2,1,0:T(1,128)S(1)}, f32[32,1,512]{2,1,0:T(1,128)S(1)}, u32[]{:S(2)}, u32[]{:S(2)}) collective-permute-start(f32[32,1,512]{2,1,0:T(1,128)S(1)} %slice.135), channel_id=1, source_target_pairs={{0,1},{1,2},{2,3},{3,4},{4,5},{5,6},{6,7},{8,9},{9,10},{10,11},{11... | collective-permute-start | bytes 196616 | tf_op jit(solution)/shard_map/ppermute | solution.py:14
  46.7 10.0 %collective-permute-start.5 = (f32[1,32,512]{2,1,0:T(8,128)S(1)}, f32[1,32,512]{2,1,0:T(8,128)S(1)}, u32[]{:S(2)}, u32[]{:S(2)}) collective-permute-start(f32[1,32,512]{2,1,0:T(8,128)S(1)} %slice.129), channel_id=1, source_target_pairs={{0,8},{8,16},{16,24},{1,9},{9,17},{17,25},{2,10},{10,18},{18,26},{... | collective-permute-start | bytes 196616 | tf_op jit(solution)/shard_map/ppermute | solution.py:14
